TPU v7x, 32 devices: a whole 2x2x4 slice. The times are simulated.
32 devices in a mesh: expert: 4 (over x, core), shard: 8 (over z, y).
Axes of the slice: x: 2, y: 2, z: 4, core: 2. Of those that a mesh axis runs over, the one named last changes fastest.
Arguments:
- master_gate: float32 [64, 2048, 1024], P('expert', 'shard'), may hold values from -0.1875 to 0.1875
- master_up: float32 [64, 2048, 1024], P('expert', 'shard'), may hold values from -0.1875 to 0.1875
- master_down: float32 [64, 1024, 2048], P('expert', None, 'shard'), may hold values from -0.25 to 0.25
- router_weight: float32 [2048, 64], P('shard', 'expert'), may hold values from -0.125 to 0.125
- router_gain: float32 [2048], P('shard'), may hold values from 0.25 to 1.75
Outputs:
- final_gate: bfloat16 [64, 2048, 1024], P('expert', None, 'shard')
- final_up: bfloat16 [64, 2048, 1024], P('expert', None, 'shard')
- final_down: bfloat16 [64, 1024, 2048], P('expert', 'shard')
- scale_gate: float32 [64, 1024], P('expert', 'shard')
- scale_up: float32 [64, 1024], P('expert', 'shard')
- scale_down: float32 [64, 1024], P('expert', 'shard')
- serve_router: bfloat16 [2048, 64], replicated
All inputs are finite; a program needn't handle non-finite values.
Results may differ from a plain program's by a relative error of at most 0.001.
Values may be sent and summed in bfloat16 or wider, within the bound.
A program may use at most 192 MiB of HBM per device.

v0:
```python
import functools

import jax
import jax.numpy as jnp
from jax import lax
from jax.experimental import pallas as pl
from jax.experimental.pallas import tpu as pltpu
from jax.sharding import PartitionSpec as P

MESH = pl.DeviceIdType.MESH
SLOTS = 4


def exchange(
    n, groups, gate, up, down, weight, gain,
    out_gate, out_up, out_down, scale_gate, scale_up, scale_down, out_router, later,
    in_gate, in_up, in_down, send_gate, send_up, send_down,
    part, arrived, owned, inverse, narrow_router,
    load_sem, part_send, part_recv, inv_send, inv_recv,
    big_send, big_recv, own_sem, router_sem,
):
    experts, rows, width = gate.shape
    early = out_down.shape[0]
    cols = width // n
    me = lax.axis_index("shard")
    grp = lax.axis_index("expert")
    order = sorted(range(1, n), key=lambda k: (abs(2 * k - n), k))
    lanes = min(128, down.shape[2])

    def peer(k):
        return lax.rem(me + k, n)

    def load(t):
        slot = lax.rem(t, SLOTS)
        return [
            pltpu.make_async_copy(src.at[t], dst.at[slot], load_sem.at[slot, i])
            for i, (src, dst) in enumerate(((gate, in_gate), (up, in_up), (down, in_down)))
        ]

    for copy in load(0):
        copy.start()

    barrier = pltpu.get_barrier_semaphore()
    for k in range(1, n):
        pl.semaphore_signal(barrier, inc=1, device_id={"shard": peer(k)}, device_id_type=MESH)
    for k in range(1, groups):
        pl.semaphore_signal(
            barrier, inc=1, device_id={"expert": lax.rem(grp + k, groups)}, device_id_type=MESH
        )

    w = weight[...]
    experts_here, depth = w.shape
    narrow_router[...] = (w * gain[...]).astype(jnp.bfloat16)
    router_rows = pl.ds(pl.multiple_of(grp * experts_here, experts_here), experts_here)
    router_cols = pl.ds(pl.multiple_of(me * depth, depth), depth)

    pl.semaphore_wait(barrier, n - 1 + groups - 1)

    def router_first(k):
        return pltpu.make_async_remote_copy(
            src_ref=narrow_router,
            dst_ref=out_router.at[router_rows, router_cols],
            send_sem=router_sem.at[0],
            recv_sem=router_sem.at[1],
            device_id={"shard": peer(k)},
            device_id_type=MESH,
        )

    router_own = pltpu.make_async_copy(
        narrow_router, out_router.at[router_rows, router_cols], router_sem.at[2]
    )

    def router_second(k):
        return pltpu.make_async_remote_copy(
            src_ref=out_router.at[router_rows, :],
            dst_ref=out_router.at[router_rows, :],
            send_sem=router_sem.at[3],
            recv_sem=router_sem.at[4],
            device_id={"expert": lax.rem(grp + k, groups)},
            device_id_type=MESH,
        )

    def sums(t):
        @pl.when(t + 1 < experts)
        def _():
            for copy in load(t + 1):
                copy.start()

        for copy in load(t):
            copy.wait()
        slot = lax.rem(t, SLOTS)
        for i, ref in enumerate((in_gate, in_up)):
            for d in range(n):
                x = ref[slot, :, d * cols:(d + 1) * cols]
                part[t, d, i] = jnp.sum(x * x, axis=0, keepdims=True)
        for d in range(n):
            x = in_down[slot, d * cols:(d + 1) * cols, :]
            x = x * x
            folded = x[:, :lanes]
            for c in range(lanes, x.shape[1], lanes):
                folded = folded + x[:, c:c + lanes]
            part[t, d, 2] = jnp.sum(folded.T, axis=0, keepdims=True)
        for k in order:
            pltpu.make_async_remote_copy(
                src_ref=part.at[t, peer(k)],
                dst_ref=arrived.at[t, k - 1],
                send_sem=part_send,
                recv_sem=part_recv.at[t],
                device_id={"shard": peer(k)},
                device_id_type=MESH,
            ).start()

    def reduce(t):
        pltpu.make_async_copy(arrived.at[t], arrived.at[t], part_recv.at[t]).wait()
        for i, out in enumerate((scale_gate, scale_up, scale_down)):
            total = part[t, me, i]
            for k in range(n - 1):
                total = total + arrived[t, k, i]
            scale = jnp.sqrt(total)
            out[pl.ds(t, 1), :] = scale
            owned[t, i] = 1.0 / scale
            inverse[t, me, i] = 1.0 / scale
        for k in order:
            pltpu.make_async_remote_copy(
                src_ref=owned.at[t],
                dst_ref=inverse.at[t, me],
                send_sem=inv_send,
                recv_sem=inv_recv.at[t],
                device_id={"shard": peer(k)},
                device_id_type=MESH,
            ).start()

    row_at = pl.ds(pl.multiple_of(me * rows, rows), rows)
    col_at = pl.ds(pl.multiple_of(me * down.shape[2], down.shape[2]), down.shape[2])

    def spread(t, i, send, place):
        for k in order:
            pltpu.make_async_remote_copy(
                src_ref=send.at[t, peer(k)],
                dst_ref=place,
                send_sem=big_send.at[i],
                recv_sem=big_recv.at[i],
                device_id={"shard": peer(k)},
                device_id_type=MESH,
            ).start()
        pltpu.make_async_copy(send.at[t, me], place, own_sem.at[i]).start()

    def finish(t):
        pltpu.make_async_copy(
            inverse.at[t, pl.ds(0, n - 1)], inverse.at[t, pl.ds(0, n - 1)], inv_recv.at[t]
        ).wait()
        slot = lax.rem(t, SLOTS)
        for i, (ref, send, out) in enumerate(
            ((in_gate, send_gate, out_gate), (in_up, send_up, out_up))
        ):
            for d in range(n):
                x = ref[slot, :, d * cols:(d + 1) * cols]
                send[t, d] = (x * inverse[t, d, i]).astype(jnp.bfloat16)
            spread(t, i, send, out.at[t, row_at, :])
        for d in range(n):
            across = jnp.broadcast_to(inverse[t, d, 2], (lanes, cols)).T
            for c in range(0, down.shape[2], lanes):
                x = in_down[slot, d * cols:(d + 1) * cols, c:c + lanes]
                send_down[t, d, :, c:c + lanes] = (x * across).astype(jnp.bfloat16)

        @pl.when(t < early)
        def _():
            spread(t, 2, send_down, out_down.at[t, :, col_at])

        @pl.when(t >= early)
        def _():
            pltpu.make_async_copy(send_down.at[t], later.at[:, t - early], own_sem.at[3]).start()

    def step(t, carry):
        @pl.when(t < experts)
        def _():
            sums(t)

        @pl.when(t == 0)
        def _():
            router_own.start()
            for k in order:
                router_first(k).start()

        @pl.when((t >= 1) & (t <= experts))
        def _():
            reduce(t - 1)

        @pl.when(t >= 2)
        def _():
            finish(t - 2)

        return carry

    lax.fori_loop(0, experts + 2, step, 0)

    router_own.wait()
    gathered = out_router.at[router_rows, pl.ds(0, (n - 1) * depth)]
    pltpu.make_async_copy(gathered, gathered, router_sem.at[1]).wait()
    for k in range(1, groups):
        router_second(k).start()

    others = pl.ds(0, n - 1)
    pltpu.make_async_copy(later, later, own_sem.at[3]).wait()
    for i, (send, sent) in enumerate(
        ((send_gate, experts), (send_up, experts), (send_down, early))
    ):
        blocks = send.at[pl.ds(0, sent), others]
        pltpu.make_async_copy(blocks, blocks, big_recv.at[i]).wait()
        pltpu.make_async_copy(blocks, blocks, big_send.at[i]).wait()
        mine = send.at[pl.ds(0, sent), 0]
        pltpu.make_async_copy(mine, mine, own_sem.at[i]).wait()
    pltpu.make_async_copy(arrived, arrived, part_send).wait()
    pltpu.make_async_copy(inverse.at[:, others], inverse.at[:, others], inv_send).wait()
    pltpu.make_async_copy(gathered, gathered, router_sem.at[0]).wait()
    handed = out_router.at[pl.ds(0, (groups - 1) * experts_here), :]
    pltpu.make_async_copy(handed, handed, router_sem.at[3]).wait()
    pltpu.make_async_copy(handed, handed, router_sem.at[4]).wait()


def by_collectives(master_gate, master_up, master_down, router_weight, router_gain):
    total_gate, total_up, total_down = lax.psum(
        (
            jnp.sum(master_gate * master_gate, axis=1),
            jnp.sum(master_up * master_up, axis=1),
            jnp.sum(master_down * master_down, axis=2),
        ),
        "shard",
    )
    scale_gate = jnp.sqrt(total_gate)
    scale_up = jnp.sqrt(total_up)
    scale_down = jnp.sqrt(total_down)
    narrow_gate, narrow_up, narrow_down = (
        (master_gate / jnp.expand_dims(scale_gate, 1)).astype(jnp.bfloat16),
        (master_up / jnp.expand_dims(scale_up, 1)).astype(jnp.bfloat16),
        (master_down / jnp.expand_dims(scale_down, 2)).astype(jnp.bfloat16),
    )
    final_gate, final_up = (
        lax.all_to_all(narrow_gate, "shard", split_axis=2, concat_axis=1, tiled=True),
        lax.all_to_all(narrow_up, "shard", split_axis=2, concat_axis=1, tiled=True),
    )
    final_down = lax.all_to_all(narrow_down, "shard", split_axis=1, concat_axis=2, tiled=True)
    scale_gate = lax.dynamic_slice_in_dim(
        scale_gate, lax.axis_index("shard") * final_gate.shape[2], final_gate.shape[2], axis=1
    )
    scale_up = lax.dynamic_slice_in_dim(
        scale_up, lax.axis_index("shard") * final_up.shape[2], final_up.shape[2], axis=1
    )
    scale_down = lax.dynamic_slice_in_dim(
        scale_down, lax.axis_index("shard") * final_down.shape[1], final_down.shape[1], axis=1
    )
    part_router = (router_weight * router_gain[:, None]).astype(jnp.bfloat16)
    row_router = lax.all_gather(part_router, "shard", axis=0, tiled=True)
    serve_router = lax.all_gather(row_router, "expert", axis=1, tiled=True)
    return (final_gate, final_up, final_down, scale_gate, scale_up, scale_down, serve_router)


def on_device(n, groups, gate, up, down, router_weight, router_gain):
    experts, rows, width = gate.shape
    cols = width // n
    inner = down.shape[2]
    depth, experts_here = router_weight.shape
    if cols % 128 or inner % 128 or depth % 128:
        return by_collectives(gate, up, down, router_weight, router_gain)
    narrow, wide = jnp.bfloat16, jnp.float32
    early = experts - max(1, experts // 8)
    dma = pltpu.SemaphoreType.DMA
    any_space = pl.BlockSpec(memory_space=pl.ANY)
    vmem = pl.BlockSpec(memory_space=pltpu.VMEM)
    outs = pl.pallas_call(
        functools.partial(exchange, n, groups),
        out_shape=(
            jax.ShapeDtypeStruct((experts, rows * n, cols), narrow),
            jax.ShapeDtypeStruct((experts, rows * n, cols), narrow),
            jax.ShapeDtypeStruct((early, cols, inner * n), narrow),
            jax.ShapeDtypeStruct((experts, cols), wide),
            jax.ShapeDtypeStruct((experts, cols), wide),
            jax.ShapeDtypeStruct((experts, cols), wide),
            jax.ShapeDtypeStruct((experts_here * groups, depth * n), narrow),
            jax.ShapeDtypeStruct((n, experts - early, cols, inner), narrow),
        ),
        in_specs=[any_space] * 3 + [vmem] * 2,
        out_specs=(any_space,) * 3 + (vmem,) * 3 + (any_space,) * 2,
        scratch_shapes=[
            pltpu.VMEM((SLOTS, rows, width), wide),
            pltpu.VMEM((SLOTS, rows, width), wide),
            pltpu.VMEM((SLOTS, width, inner), wide),
            pltpu.VMEM((experts, n, rows, cols), narrow),
            pltpu.VMEM((experts, n, rows, cols), narrow),
            pltpu.VMEM((experts, n, cols, inner), narrow),
            pltpu.VMEM((experts, n, 3, 1, cols), wide),
            pltpu.VMEM((experts, n - 1, 3, 1, cols), wide),
            pltpu.VMEM((experts, 3, 1, cols), wide),
            pltpu.VMEM((experts, n, 3, 1, cols), wide),
            pltpu.VMEM((experts_here, depth), narrow),
            dma((SLOTS, 3)),
            dma,
            dma((experts,)),
            dma,
            dma((experts,)),
            dma((3,)),
            dma((3,)),
            dma((4,)),
            dma((5,)),
        ],
        compiler_params=pltpu.CompilerParams(
            collective_id=0, has_side_effects=True, vmem_limit_bytes=60 * 2**20
        ),
    )(gate, up, down, router_weight.T, router_gain[None, :])
    late = lax.all_to_all(outs[7], "shard", split_axis=0, concat_axis=0, tiled=True)

    def one(shape, cap):
        block = (1,) + shape[1:]
        return pl.BlockSpec(block, lambda t: (jnp.minimum(t, cap - 1), 0, 0))

    specs = [
        one(outs[0].shape, experts),
        one(outs[1].shape, experts),
        one(outs[2].shape, early),
    ] + [pl.BlockSpec(x.shape, lambda t: (0, 0)) for x in outs[3:7]]
    full = jax.ShapeDtypeStruct((experts, cols, inner * n), narrow)
    moved = sum(x.size * x.dtype.itemsize for x in outs[:7])
    placed = pl.pallas_call(
        place,
        grid=(experts,),
        in_specs=specs,
        out_specs=specs,
        out_shape=tuple(
            full if i == 2 else jax.ShapeDtypeStruct(x.shape, x.dtype)
            for i, x in enumerate(outs[:7])
        ),
        compiler_params=pltpu.CompilerParams(dimension_semantics=("arbitrary",)),
        cost_estimate=pl.CostEstimate(flops=0, bytes_accessed=2 * moved, transcendentals=0),
    )(*outs[:7])
    final_down = pl.pallas_call(
        functools.partial(place_late, n, early),
        in_specs=[any_space] * 2,
        out_specs=any_space,
        out_shape=full,
        input_output_aliases={0: 0},
        scratch_shapes=[dma((n,))],
        compiler_params=pltpu.CompilerParams(vmem_limit_bytes=2**20),
    )(placed[2], late)
    return placed[:2] + (final_down,) + placed[3:6] + (placed[6].T,)


def place(*refs):
    half = len(refs) // 2
    for src, dst in zip(refs[:half], refs[half:]):
        dst[...] = src[...]


def place_late(n, early, _, late, out, sem):
    inner = late.shape[3]
    copies = [
        pltpu.make_async_copy(
            late.at[d],
            out.at[pl.ds(early, late.shape[1]), :, pl.ds(d * inner, inner)],
            sem.at[d],
        )
        for d in range(n)
    ]
    for copy in copies:
        copy.start()
    for copy in copies:
        copy.wait()


def solution(mesh):
    placed = (
        P("expert", "shard", None),
        P("expert", "shard", None),
        P("expert", None, "shard"),
        P("shard", "expert"),
        P("shard"),
    )
    return jax.shard_map(
        functools.partial(on_device, mesh.shape["shard"], mesh.shape["expert"]),
        mesh=mesh,
        in_specs=placed,
        out_specs=(
            P("expert", None, "shard"),
            P("expert", None, "shard"),
            P("expert", "shard", None),
            P("expert", "shard"),
            P("expert", "shard"),
            P("expert", "shard"),
            P(),
        ),
        check_vma=False,
    )
```

profile of v0, /device:TPU:0, one launch (start us, length us, event | category | flops | bytes accessed | tf_op | source)
XLA Modules:
  0.0 570.0 jit_solution(12858681172371220265)
XLA Ops:
  0.6 539.1 %shard_map.108 = (bf16[16,2048,128]{2,1,0:T(8,128)(2,1)}, bf16[16,2048,128]{2,1,0:T(8,128)(2,1)}, bf16[14,128,2048]{2,1,0:T(8,128)(2,1)}, f32[16,128]{1,0:T(8,12...) custom-call(f32[16,256,1024]{2,1,0:T(8,128)} %gate.1, ...), custom_call_target="tpu_custom_call" | custom-call | tf_op jit(solution)/shard_map/pallas_call | solution.py:270
  539.7 4.5 all-to-all-start
  544.2 21.7 %shard_map.109 = (bf16[16,2048,128]{2,1,0:T(8,128)(2,1)}, bf16[16,2048,128]{2,1,0:T(8,128)(2,1)}, bf16[16,128,2048]{2,1,0:T(8,128)(2,1)}, f32[16,128]{1,0:T(8,12...) custom-call(bf16[16,2048,128]{2,1,0:T(8,128)(2,1)} %get-tuple-element.22.refs_0_, ...), custom_call_target="tpu_custom_call" | custom-call | bytes 48807936 | tf_op jit(solution)/shard_map/pallas_call | solution.py:323
  565.9 3.1 all-to-all-done.late
  569.0 1.0 shard_map.110
Async XLA Ops:
  539.7 29.2 %all-to-all-start = ((bf16[8,2,128,256]{3,2,1,0:T(8,128)(2,1)}), bf16[8,2,128,256]{3,2,1,0:T(8,128)(2,1)S(1)}, u32[]{:S(2)}, u32[]{:S(2)}) async-start(bf16[8,2,128,256]{3,2,1,0:T(8,128)(2,1)} %get-tuple-element.32), calls=%async_computation | async-start | bytes 2097152 | tf_op jit(solution)/shard_map/all_to_all | solution.py:310
where the time goes:
time: 571 us; the launch traced here: 570 us
  Pallas kernels  562 us (98%)
    pallas_call x1, Pallas kernels, on_device(): pl.pallas_call(functools.partial(exchange, n, groups), out_shape=(jax.Sha...  539 us
    pallas_call x1, Pallas kernels, on_device(): pl.pallas_call(place, grid=(experts,), in_specs=specs, out_specs=specs, o...  21.7 us
  transfers between devices with their start and end apart: 1, of which 1 were waited for; matrix products, arithmetic and copies ran while one was open for 0% of the time, Pallas kernels for 4%

commit v1 on v0

v1 whole, which is shorter than its diff:
```python
import functools

import jax
import jax.numpy as jnp
from jax import lax
from jax.experimental import pallas as pl
from jax.experimental.pallas import tpu as pltpu
from jax.sharding import PartitionSpec as P

MESH = pl.DeviceIdType.MESH
SLOTS = 6
EARLY = (0, 1, 2, 0)


def exchange(
    n, groups, late, gate, up, down, weight, gain,
    out_gate, out_up, out_down, scale_gate, scale_up, scale_down, out_router, later,
    in_gate, in_up, in_down, send_gate, send_up, send_down, raw_wide, raw_down,
    part, arrived, mine, crossed, owned, inverse, narrow_router,
    load_sem, half_send, half_recv, cross_send, cross_recv, inv_send, inv_recv,
    big_send, big_recv, own_sem, later_sem, raw_send, raw_recv, raw_out, router_sem,
):
    experts, rows, width = gate.shape
    cols = width // n
    inner = down.shape[2]
    half = n // 2
    first_late = experts - late
    lanes = min(128, inner)
    me = lax.axis_index("shard")
    grp = lax.axis_index("expert")
    side, place = me // half, me % half

    def at(across, step):
        there = lax.rem(side + across, 2)
        q = lax.rem(place + step, half)
        return there, q, there * half + q

    order = []
    for r in range(half):
        order.append((1, r))
        if half - 1 - r > 0:
            order.append((0, half - 1 - r))

    def load(t):
        slot = lax.rem(t, SLOTS)
        return [
            pltpu.make_async_copy(src.at[t], dst.at[slot], load_sem.at[slot, i])
            for i, (src, dst) in enumerate(((gate, in_gate), (up, in_up), (down, in_down)))
        ]

    for t in range(2):
        for copy in load(t):
            copy.start()

    barrier = pltpu.get_barrier_semaphore()
    for k in range(1, n):
        pl.semaphore_signal(
            barrier, inc=1, device_id={"shard": lax.rem(me + k, n)}, device_id_type=MESH
        )
    for k in range(1, groups):
        pl.semaphore_signal(
            barrier, inc=1, device_id={"expert": lax.rem(grp + k, groups)}, device_id_type=MESH
        )

    w = weight[...]
    experts_here, depth = w.shape
    narrow_router[...] = (w * gain[...]).astype(jnp.bfloat16)
    router_rows = pl.ds(pl.multiple_of(grp * experts_here, experts_here), experts_here)

    def router_block(d):
        return out_router.at[router_rows, pl.ds(pl.multiple_of(d * depth, depth), depth)]

    row_at = pl.ds(pl.multiple_of(me * rows, rows), rows)
    col_at = pl.ds(pl.multiple_of(me * inner, inner), inner)

    def router_first(across, step, sem):
        return pltpu.make_async_remote_copy(
            src_ref=narrow_router,
            dst_ref=router_block(me),
            send_sem=router_sem.at[0],
            recv_sem=router_sem.at[sem],
            device_id={"shard": at(across, step)[2]},
            device_id_type=MESH,
        )

    router_own = pltpu.make_async_copy(narrow_router, router_block(me), router_sem.at[2])

    def router_relay(step):
        across = router_block(at(1, 0)[2])
        return pltpu.make_async_remote_copy(
            src_ref=across,
            dst_ref=across,
            send_sem=router_sem.at[0],
            recv_sem=router_sem.at[1],
            device_id={"shard": at(0, step)[2]},
            device_id_type=MESH,
        )

    def router_second(k):
        return pltpu.make_async_remote_copy(
            src_ref=out_router.at[router_rows, :],
            dst_ref=out_router.at[router_rows, :],
            send_sem=router_sem.at[3],
            recv_sem=router_sem.at[4],
            device_id={"expert": lax.rem(grp + k, groups)},
            device_id_type=MESH,
        )

    def block_of(ref, slot, d):
        return ref[slot, :, pl.ds(pl.multiple_of(d * cols, cols), cols)]

    def raw_copy(r):
        i = EARLY[r % len(EARLY)]
        d = at(1, r)[2]
        return pltpu.make_async_remote_copy(
            src_ref=(send_gate, send_up, send_down)[i].at[d],
            dst_ref=raw_down.at[r] if i == 2 else raw_wide.at[r],
            send_sem=raw_send.at[r],
            recv_sem=raw_recv.at[r],
            device_id={"shard": d},
            device_id_type=MESH,
        )

    def raw_fill(r):
        i = EARLY[r % len(EARLY)]
        d = at(1, r)[2]
        if i == 2:
            x = in_down[0, pl.ds(pl.multiple_of(d * cols, cols), cols), :]
        else:
            x = block_of((in_gate, in_up)[i], 0, d)
        (send_gate, send_up, send_down)[i][d] = x.astype(jnp.bfloat16)

    def down_factor(q, h, t):
        return jnp.broadcast_to(inverse[t, q, h, 2], (lanes, cols)).T

    def raw_out_copy(r):
        s = at(1, half - r)[2]
        i = EARLY[r % len(EARLY)]
        if i == 2:
            to = out_down.at[0, :, pl.ds(pl.multiple_of(s * inner, inner), inner)]
            return pltpu.make_async_copy(raw_down.at[r], to, raw_out.at[r])
        to = (out_gate, out_up)[i].at[0, pl.ds(pl.multiple_of(s * rows, rows), rows), :]
        return pltpu.make_async_copy(raw_wide.at[r], to, raw_out.at[r])

    def raw_scale(r):
        i = EARLY[r % len(EARLY)]
        raw_copy(r).wait_recv()
        if i == 2:
            factor = down_factor(place, side, 0)
            for c in range(0, inner, lanes):
                x = raw_down[r, :, c:c + lanes].astype(jnp.float32)
                raw_down[r, :, c:c + lanes] = (x * factor).astype(jnp.bfloat16)
        else:
            x = raw_wide[r].astype(jnp.float32)
            raw_wide[r] = (x * inverse[0, place, side, i]).astype(jnp.bfloat16)

    def sums(t):
        slot = lax.rem(t, SLOTS)
        for d in range(n):
            h, q = d // half, d % half
            for i, ref in enumerate((in_gate, in_up)):
                x = ref[slot, :, d * cols:(d + 1) * cols]
                part[t, q, h, i] = jnp.sum(x * x, axis=0, keepdims=True)
            x = in_down[slot, d * cols:(d + 1) * cols, :]
            x = x * x
            folded = x[:, :lanes]
            for c in range(lanes, inner, lanes):
                folded = folded + x[:, c:c + lanes]
            part[t, q, h, 2] = jnp.sum(folded.T, axis=0, keepdims=True)
        for k in range(1, half):
            _, q, d = at(0, k)
            pltpu.make_async_remote_copy(
                src_ref=part.at[t, q],
                dst_ref=arrived.at[t, k - 1],
                send_sem=half_send,
                recv_sem=half_recv.at[t],
                device_id={"shard": d},
                device_id_type=MESH,
            ).start()

    def cross_copy(t):
        return pltpu.make_async_remote_copy(
            src_ref=mine.at[t],
            dst_ref=crossed.at[t],
            send_sem=cross_send,
            recv_sem=cross_recv.at[t],
            device_id={"shard": at(1, 0)[2]},
            device_id_type=MESH,
        )

    def cross(t):
        pltpu.make_async_copy(arrived.at[t], arrived.at[t], half_recv.at[t]).wait()
        total = part[t, place]
        for k in range(half - 1):
            total = total + arrived[t, k]
        mine[t] = total
        cross_copy(t).start()

    def reduce(t):
        cross_copy(t).wait_recv()
        for i, out in enumerate((scale_gate, scale_up, scale_down)):
            out[pl.ds(t, 1), :] = jnp.sqrt(mine[t, side, i] + crossed[t, side, i])
        scaled = 1.0 / jnp.sqrt(mine[t] + crossed[t])
        owned[t] = scaled
        inverse[t, place] = scaled
        for k in range(1, half):
            pltpu.make_async_remote_copy(
                src_ref=owned.at[t],
                dst_ref=inverse.at[t, place],
                send_sem=inv_send,
                recv_sem=inv_recv.at[t],
                device_id={"shard": at(0, k)[2]},
                device_id_type=MESH,
            ).start()

    def finish(t, first):
        others = pl.ds(0, half - 1)
        pltpu.make_async_copy(
            inverse.at[t, others], inverse.at[t, others], inv_recv.at[t]
        ).wait()
        slot = lax.rem(t, SLOTS)
        for i, (ref, send, place_at) in enumerate((
            (in_gate, send_gate, out_gate.at[t, row_at, :]),
            (in_up, send_up, out_up.at[t, row_at, :]),
            (in_down, send_down, out_down.at[t, :, col_at]),
        )):
            waiting = None
            for across, step in order + [(0, 0)]:
                if first and across == 1 and EARLY[step % len(EARLY)] == i:
                    continue
                h, q, d = at(across, step)
                to = t * n + d
                if i == 2:
                    factor = down_factor(q, h, t)
                    for c in range(0, inner, lanes):
                        x = ref[slot, pl.ds(pl.multiple_of(d * cols, cols), cols), c:c + lanes]
                        send[to, :, c:c + lanes] = (x * factor).astype(jnp.bfloat16)
                else:
                    x = block_of(ref, slot, d)
                    send[to] = (x * inverse[t, q, h, i]).astype(jnp.bfloat16)
                if waiting is not None:
                    waiting()

                def go(across=across, step=step, d=d, to=to):
                    if (across, step) == (0, 0):
                        pltpu.make_async_copy(send.at[to], place_at, own_sem.at[i]).start()
                        return
                    copy = pltpu.make_async_remote_copy(
                        src_ref=send.at[to],
                        dst_ref=place_at,
                        send_sem=big_send.at[i],
                        recv_sem=big_recv.at[i],
                        device_id={"shard": d},
                        device_id_type=MESH,
                    )
                    if i == 2 and (across, step) == (1, 0) and not first:
                        @pl.when(t < first_late)
                        def _():
                            copy.start()

                        @pl.when(t >= first_late)
                        def _():
                            pltpu.make_async_copy(
                                send.at[to], later.at[t - first_late], later_sem
                            ).start()
                    else:
                        copy.start()

                waiting = go
            waiting()

    def step(t, carry):
        @pl.when(t + 2 < experts)
        def _():
            for copy in load(t + 2):
                copy.start()

        @pl.when(t < experts)
        def _():
            for copy in load(t):
                copy.wait()
            sums(t)

        @pl.when((t >= 1) & (t <= experts))
        def _():
            cross(t - 1)

        @pl.when(t == 2)
        def _():
            for r in range(half // 2, half):
                raw_copy(r).start()

        @pl.when((t >= 2) & (t <= experts + 1))
        def _():
            reduce(t - 2)

        @pl.when(t == 3)
        def _():
            router_first(1, 0, 5).wait_recv()
            for k in range(1, half):
                router_relay(k).start()
            finish(0, True)
            for r in range(half):
                raw_scale(r)
                if r:
                    raw_out_copy(r - 1).start()
            raw_out_copy(half - 1).start()

        @pl.when(t > 3)
        def _():
            finish(t - 3, False)

        return carry

    for copy in load(2):
        copy.start()
    for copy in load(0):
        copy.wait()
    for r in range(half):
        raw_fill(r)
    pl.semaphore_wait(barrier, n - 1 + groups - 1)
    sums(0)
    router_own.start()
    for k in range(1, half):
        router_first(0, k, 1).start()
    router_first(1, 0, 5).start()
    for r in range(half // 2):
        raw_copy(r).start()
    lax.fori_loop(1, experts + 3, step, 0)

    gathered = out_router.at[router_rows, pl.ds(0, (n - 1) * depth)]
    near = out_router.at[router_rows, pl.ds(0, (n - 2) * depth)]
    router_own.wait()
    pltpu.make_async_copy(near, near, router_sem.at[1]).wait()
    for k in range(1, groups):
        router_second(k).start()

    pltpu.make_async_copy(later, later, later_sem).wait()
    for r in range(half):
        raw_copy(r).wait_send()
        raw_out_copy(r).wait()
    for i, send in enumerate((send_gate, send_up, send_down)):
        sent = experts * (n - 1) - sum(EARLY[r % len(EARLY)] == i for r in range(half))
        if i == 2:
            sent -= late
        blocks = send.at[pl.ds(0, sent)]
        pltpu.make_async_copy(blocks, blocks, big_recv.at[i]).wait()
        pltpu.make_async_copy(blocks, blocks, big_send.at[i]).wait()
        kept = send.at[pl.ds(0, experts)]
        pltpu.make_async_copy(kept, kept, own_sem.at[i]).wait()
    pltpu.make_async_copy(arrived, arrived, half_send).wait()
    pltpu.make_async_copy(crossed, crossed, cross_send).wait()
    others = pl.ds(0, half - 1)
    pltpu.make_async_copy(inverse.at[:, others], inverse.at[:, others], inv_send).wait()
    pltpu.make_async_copy(gathered, gathered, router_sem.at[0]).wait()
    handed = out_router.at[pl.ds(0, (groups - 1) * experts_here), :]
    pltpu.make_async_copy(handed, handed, router_sem.at[3]).wait()
    pltpu.make_async_copy(handed, handed, router_sem.at[4]).wait()


def by_collectives(master_gate, master_up, master_down, router_weight, router_gain):
    total_gate, total_up, total_down = lax.psum(
        (
            jnp.sum(master_gate * master_gate, axis=1),
            jnp.sum(master_up * master_up, axis=1),
            jnp.sum(master_down * master_down, axis=2),
        ),
        "shard",
    )
    scale_gate = jnp.sqrt(total_gate)
    scale_up = jnp.sqrt(total_up)
    scale_down = jnp.sqrt(total_down)
    narrow_gate, narrow_up, narrow_down = (
        (master_gate / jnp.expand_dims(scale_gate, 1)).astype(jnp.bfloat16),
        (master_up / jnp.expand_dims(scale_up, 1)).astype(jnp.bfloat16),
        (master_down / jnp.expand_dims(scale_down, 2)).astype(jnp.bfloat16),
    )
    final_gate, final_up = (
        lax.all_to_all(narrow_gate, "shard", split_axis=2, concat_axis=1, tiled=True),
        lax.all_to_all(narrow_up, "shard", split_axis=2, concat_axis=1, tiled=True),
    )
    final_down = lax.all_to_all(narrow_down, "shard", split_axis=1, concat_axis=2, tiled=True)
    scale_gate = lax.dynamic_slice_in_dim(
        scale_gate, lax.axis_index("shard") * final_gate.shape[2], final_gate.shape[2], axis=1
    )
    scale_up = lax.dynamic_slice_in_dim(
        scale_up, lax.axis_index("shard") * final_up.shape[2], final_up.shape[2], axis=1
    )
    scale_down = lax.dynamic_slice_in_dim(
        scale_down, lax.axis_index("shard") * final_down.shape[1], final_down.shape[1], axis=1
    )
    part_router = (router_weight * router_gain[:, None]).astype(jnp.bfloat16)
    row_router = lax.all_gather(part_router, "shard", axis=0, tiled=True)
    serve_router = lax.all_gather(row_router, "expert", axis=1, tiled=True)
    return (final_gate, final_up, final_down, scale_gate, scale_up, scale_down, serve_router)


def on_device(n, groups, gate, up, down, router_weight, router_gain):
    experts, rows, width = gate.shape
    cols = width // n
    inner = down.shape[2]
    depth, experts_here = router_weight.shape
    if cols % 128 or inner % 128 or depth % 128 or n % 2 or n < 4 or experts < 8:
        return by_collectives(gate, up, down, router_weight, router_gain)
    narrow, wide = jnp.bfloat16, jnp.float32
    half = n // 2
    late = experts // 2
    dma = pltpu.SemaphoreType.DMA
    any_space = pl.BlockSpec(memory_space=pl.ANY)
    vmem = pl.BlockSpec(memory_space=pltpu.VMEM)
    outs = pl.pallas_call(
        functools.partial(exchange, n, groups, late),
        out_shape=(
            jax.ShapeDtypeStruct((experts, rows * n, cols), narrow),
            jax.ShapeDtypeStruct((experts, rows * n, cols), narrow),
            jax.ShapeDtypeStruct((experts, cols, inner * n), narrow),
            jax.ShapeDtypeStruct((experts, cols), wide),
            jax.ShapeDtypeStruct((experts, cols), wide),
            jax.ShapeDtypeStruct((experts, cols), wide),
            jax.ShapeDtypeStruct((experts_here * groups, depth * n), narrow),
            jax.ShapeDtypeStruct((late, cols, inner), narrow),
        ),
        in_specs=[any_space] * 3 + [vmem] * 2,
        out_specs=(any_space,) * 3 + (vmem,) * 3 + (any_space,) * 2,
        scratch_shapes=[
            pltpu.VMEM((SLOTS, rows, width), wide),
            pltpu.VMEM((SLOTS, rows, width), wide),
            pltpu.VMEM((SLOTS, width, inner), wide),
            pltpu.VMEM((experts * n, rows, cols), narrow),
            pltpu.VMEM((experts * n, rows, cols), narrow),
            pltpu.VMEM((experts * n, cols, inner), narrow),
            pltpu.VMEM((half, rows, cols), narrow),
            pltpu.VMEM((half, cols, inner), narrow),
            pltpu.VMEM((experts, half, 2, 3, 1, cols), wide),
            pltpu.VMEM((experts, half - 1, 2, 3, 1, cols), wide),
            pltpu.VMEM((experts, 2, 3, 1, cols), wide),
            pltpu.VMEM((experts, 2, 3, 1, cols), wide),
            pltpu.VMEM((experts, 2, 3, 1, cols), wide),
            pltpu.VMEM((experts, half, 2, 3, 1, cols), wide),
            pltpu.VMEM((experts_here, depth), narrow),
            dma((SLOTS, 3)),
            dma,
            dma((experts,)),
            dma,
            dma((experts,)),
            dma,
            dma((experts,)),
            dma((3,)),
            dma((3,)),
            dma((3,)),
            dma,
            dma((half,)),
            dma((half,)),
            dma((half,)),
            dma((6,)),
        ],
        compiler_params=pltpu.CompilerParams(
            collective_id=0, has_side_effects=True, vmem_limit_bytes=60 * 2**20
        ),
    )(gate, up, down, router_weight.T, router_gain[None, :])
    swap = [(d, (d + half) % n) for d in range(n)]
    late_blocks = lax.ppermute(outs[7], "shard", swap)

    def one(shape):
        return pl.BlockSpec((1,) + shape[1:], lambda t: (t, 0, 0))

    specs = [one(x.shape) for x in outs[:3]]
    specs += [pl.BlockSpec(x.shape, lambda t: (0, 0)) for x in outs[3:7]]
    moved = sum(x.size * x.dtype.itemsize for x in outs[:7])
    placed = pl.pallas_call(
        place,
        grid=(experts,),
        in_specs=specs,
        out_specs=specs,
        out_shape=tuple(jax.ShapeDtypeStruct(x.shape, x.dtype) for x in outs[:7]),
        compiler_params=pltpu.CompilerParams(dimension_semantics=("arbitrary",)),
        cost_estimate=pl.CostEstimate(flops=0, bytes_accessed=2 * moved, transcendentals=0),
    )(*outs[:7])
    final_down = pl.pallas_call(
        functools.partial(place_late, n),
        in_specs=[any_space] * 2,
        out_specs=any_space,
        out_shape=jax.ShapeDtypeStruct(outs[2].shape, narrow),
        input_output_aliases={0: 0},
        scratch_shapes=[dma],
        compiler_params=pltpu.CompilerParams(vmem_limit_bytes=2**20),
    )(placed[2], late_blocks)
    return placed[:2] + (final_down,) + placed[3:6] + (placed[6].T,)


def place(*refs):
    half = len(refs) // 2
    for src, dst in zip(refs[:half], refs[half:]):
        dst[...] = src[...]


def place_late(n, _, late, out, sem):
    count, _, inner = late.shape
    source = lax.rem(lax.axis_index("shard") + n // 2, n)
    cols = pl.ds(pl.multiple_of(source * inner, inner), inner)
    copy = pltpu.make_async_copy(
        late, out.at[pl.ds(out.shape[0] - count, count), :, cols], sem
    )
    copy.start()
    copy.wait()


def solution(mesh):
    placed = (
        P("expert", "shard", None),
        P("expert", "shard", None),
        P("expert", None, "shard"),
        P("shard", "expert"),
        P("shard"),
    )
    return jax.shard_map(
        functools.partial(on_device, mesh.shape["shard"], mesh.shape["expert"]),
        mesh=mesh,
        in_specs=placed,
        out_specs=(
            P("expert", None, "shard"),
            P("expert", None, "shard"),
            P("expert", "shard", None),
            P("expert", "shard"),
            P("expert", "shard"),
            P("expert", "shard"),
            P(),
        ),
        check_vma=False,
    )
```

time: 571 us -> 556 us (0.974)
  Pallas kernels: 562 us -> 555 us
    pallas_call x2, Pallas kernels: 540 us -> 532 us  [the longest x1 531 us: on_device(): pl.pallas_call(functools.partial(exchange, n, groups, late), out_shape=(j...]
  transfers between devices with their start and end apart: 1 -> 1, of which waited for: 1 -> 0; matrix products, arithmetic and copies ran while one was open for 0% -> 0% of each run, Pallas kernels for 4% -> 4%
where the time goes in v1:
time: 556 us; the launch traced here: 555 us
  Pallas kernels  555 us (100%)
    pallas_call x1, Pallas kernels, on_device(): pl.pallas_call(functools.partial(exchange, n, groups, late), out_shape=(j...  531 us
    pallas_call x1, Pallas kernels, on_device(): pl.pallas_call(place, grid=(experts,), in_specs=specs, out_specs=specs, o...  22.3 us
  transfers between devices with their start and end apart: 1, of which 0 were waited for; matrix products, arithmetic and copies ran while one was open for 0% of the time, Pallas kernels for 4%

profile of v1, /device:TPU:0, one launch (start us, length us, event | category | flops | bytes accessed | tf_op | source)
XLA Modules:
  0.0 555.3 jit_solution(15979442853354034601)
XLA Ops:
  0.6 531.4 %shard_map.108 = (bf16[16,2048,128]{2,1,0:T(8,128)(2,1)}, bf16[16,2048,128]{2,1,0:T(8,128)(2,1)}, bf16[16,128,2048]{2,1,0:T(8,128)(2,1)}, f32[16,128]{1,0:T(8,12...) custom-call(f32[16,256,1024]{2,1,0:T(8,128)} %gate.1, ...), custom_call_target="tpu_custom_call" | custom-call | tf_op jit(solution)/shard_map/pallas_call | solution.py:411
  532.1 0.1 collective-permute-start
  532.2 22.3 %shard_map.109 = (bf16[16,2048,128]{2,1,0:T(8,128)(2,1)}, bf16[16,2048,128]{2,1,0:T(8,128)(2,1)}, bf16[16,128,2048]{2,1,0:T(8,128)(2,1)}, f32[16,128]{1,0:T(8,12...) custom-call(bf16[16,2048,128]{2,1,0:T(8,128)(2,1)} %get-tuple-element.22.refs_0_, ...), custom_call_target="tpu_custom_call" | custom-call | bytes 50905088 | tf_op jit(solution)/shard_map/pallas_call | solution.py:470
  554.5 0.0 collective-permute-done.late
  554.5 0.8 shard_map.110
Async XLA Ops:
  532.1 22.4 %collective-permute-start = (bf16[8,128,256]{2,1,0:T(8,128)(2,1)}, bf16[8,128,256]{2,1,0:T(8,128)(2,1)S(1)}, u32[]{:S(2)}, u32[]{:S(2)}) collective-permute-start(bf16[8,128,256]{2,1,0:T(8,128)(2,1)} %get-tuple-element.32), channel_id=1, source_target_pairs={{0,4},{1,5},{2,6},{3,7},{4,0},{5,1},{6,2},{7,3},{8,12},{9,13},{10,... | collective-permute-start | bytes 1572872 | tf_op jit(solution)/shard_map/ppermute | solution.py:462

commit v2 on v1

--- a/solution.py
+++ b/solution.py
@@ -167,6 +167,8 @@
             for c in range(lanes, inner, lanes):
                 folded = folded + x[:, c:c + lanes]
             part[t, q, h, 2] = jnp.sum(folded.T, axis=0, keepdims=True)
+
+    def share(t):
         for k in range(1, half):
             _, q, d = at(0, k)
             pltpu.make_async_remote_copy(
@@ -253,7 +255,7 @@
                         device_id={"shard": d},
                         device_id_type=MESH,
                     )
-                    if i == 2 and (across, step) == (1, 0) and not first:
+                    if i == 2 and (across, step) == (1, half // 2) and not first:
                         @pl.when(t < first_late)
                         def _():
                             copy.start()
@@ -280,6 +282,7 @@
             for copy in load(t):
                 copy.wait()
             sums(t)
+            share(t)
 
         @pl.when((t >= 1) & (t <= experts))
         def _():
@@ -318,8 +321,9 @@
         copy.wait()
     for r in range(half):
         raw_fill(r)
+    sums(0)
     pl.semaphore_wait(barrier, n - 1 + groups - 1)
-    sums(0)
+    share(0)
     router_own.start()
     for k in range(1, half):
         router_first(0, k, 1).start()
@@ -404,7 +408,7 @@
         return by_collectives(gate, up, down, router_weight, router_gain)
     narrow, wide = jnp.bfloat16, jnp.float32
     half = n // 2
-    late = experts // 2
+    late = experts * 8 // 16
     dma = pltpu.SemaphoreType.DMA
     any_space = pl.BlockSpec(memory_space=pl.ANY)
     vmem = pl.BlockSpec(memory_space=pltpu.VMEM)
@@ -458,22 +462,20 @@
             collective_id=0, has_side_effects=True, vmem_limit_bytes=60 * 2**20
         ),
     )(gate, up, down, router_weight.T, router_gain[None, :])
-    swap = [(d, (d + half) % n) for d in range(n)]
+    swap = [(d, n - half * (d // half + 1) + (d + half // 2) % half) for d in range(n)]
     late_blocks = lax.ppermute(outs[7], "shard", swap)
 
-    def one(shape):
-        return pl.BlockSpec((1,) + shape[1:], lambda t: (t, 0, 0))
-
-    specs = [one(x.shape) for x in outs[:3]]
-    specs += [pl.BlockSpec(x.shape, lambda t: (0, 0)) for x in outs[3:7]]
+    big = [jax.ShapeDtypeStruct(x.shape, x.dtype) for x in outs[:3]]
+    small = [jax.ShapeDtypeStruct(x.shape, x.dtype) for x in outs[3:7]]
     moved = sum(x.size * x.dtype.itemsize for x in outs[:7])
     placed = pl.pallas_call(
         place,
-        grid=(experts,),
-        in_specs=specs,
-        out_specs=specs,
-        out_shape=tuple(jax.ShapeDtypeStruct(x.shape, x.dtype) for x in outs[:7]),
-        compiler_params=pltpu.CompilerParams(dimension_semantics=("arbitrary",)),
+        in_specs=[any_space] * 3 + [vmem] * 4,
+        out_specs=[any_space] * 3 + [vmem] * 4,
+        out_shape=big + small,
+        scratch_shapes=[pltpu.VMEM(x.shape, x.dtype) for x in big]
+        + [dma((3, experts)), dma((3, experts))],
+        compiler_params=pltpu.CompilerParams(vmem_limit_bytes=60 * 2**20),
         cost_estimate=pl.CostEstimate(flops=0, bytes_accessed=2 * moved, transcendentals=0),
     )(*outs[:7])
     final_down = pl.pallas_call(
@@ -485,18 +487,34 @@
         scratch_shapes=[dma],
         compiler_params=pltpu.CompilerParams(vmem_limit_bytes=2**20),
     )(placed[2], late_blocks)
-    return placed[:2] + (final_down,) + placed[3:6] + (placed[6].T,)
+    return tuple(placed[:2]) + (final_down,) + tuple(placed[3:6]) + (placed[6].T,)
 
 
 def place(*refs):
-    half = len(refs) // 2
-    for src, dst in zip(refs[:half], refs[half:]):
+    srcs, dsts, held, taken, given = refs[:7], refs[7:14], refs[14:17], refs[17], refs[18]
+    pairs = [(t, i) for t in range(srcs[0].shape[0]) for i in range(3)]
+
+    def take(t, i):
+        return pltpu.make_async_copy(srcs[i].at[t], held[i].at[t], taken.at[i, t])
+
+    def give(t, i):
+        return pltpu.make_async_copy(held[i].at[t], dsts[i].at[t], given.at[i, t])
+
+    for t, i in pairs:
+        take(t, i).start()
+    for src, dst in zip(srcs[3:], dsts[3:]):
         dst[...] = src[...]
+    for t, i in pairs:
+        take(t, i).wait()
+        give(t, i).start()
+    for t, i in pairs:
+        give(t, i).wait()
 
 
 def place_late(n, _, late, out, sem):
     count, _, inner = late.shape
-    source = lax.rem(lax.axis_index("shard") + n // 2, n)
+    me, half = lax.axis_index("shard"), n // 2
+    source = (1 - me // half) * half + lax.rem(me + half // 2, half)
     cols = pl.ds(pl.multiple_of(source * inner, inner), inner)
     copy = pltpu.make_async_copy(
         late, out.at[pl.ds(out.shape[0] - count, count), :, cols], sem

time: 556 us -> 554 us (level)
  transfers between devices with their start and end apart: 1 -> 1, of which waited for: 0 -> 0; matrix products, arithmetic and copies ran while one was open for 0% -> 0% of each run, Pallas kernels for 4% -> 3%
where the time goes in v2:
time: 554 us; the launch traced here: 553 us
  Pallas kernels  551 us (99%)
    pallas_call x1, Pallas kernels, on_device(): pl.pallas_call(functools.partial(exchange, n, groups, late), out_shape=(j...  531 us
    pallas_call x1, Pallas kernels, on_device(): pl.pallas_call(place, in_specs=[any_space] * 3 + [vmem] * 4, out_specs=[a...  19.3 us
  transfers between devices with their start and end apart: 1, of which 0 were waited for; matrix products, arithmetic and copies ran while one was open for 0% of the time, Pallas kernels for 3%

profile of v2, /device:TPU:0, one launch (start us, length us, event | category | flops | bytes accessed | tf_op | source)
XLA Modules:
  0.0 553.4 jit_solution(12006036248927240794)
XLA Ops:
  0.6 530.9 %shard_map.108 = (bf16[16,2048,128]{2,1,0:T(8,128)(2,1)}, bf16[16,2048,128]{2,1,0:T(8,128)(2,1)}, bf16[16,128,2048]{2,1,0:T(8,128)(2,1)}, f32[16,128]{1,0:T(8,12...) custom-call(f32[16,256,1024]{2,1,0:T(8,128)} %gate.1, ...), custom_call_target="tpu_custom_call" | custom-call | tf_op jit(solution)/shard_map/pallas_call | solution.py:415
  531.5 1.7 collective-permute-start
  533.3 19.3 %shard_map.109 = (bf16[16,2048,128]{2,1,0:T(8,128)(2,1)}, bf16[16,2048,128]{2,1,0:T(8,128)(2,1)}, bf16[16,128,2048]{2,1,0:T(8,128)(2,1)}, f32[16,128]{1,0:T(8,12...) custom-call(bf16[16,2048,128]{2,1,0:T(8,128)(2,1)} %get-tuple-element.22.refs_0_, ...), custom_call_target="tpu_custom_call" | custom-call | bytes 50905088 | tf_op jit(solution)/shard_map/pallas_call | solution.py:471
  552.6 0.0 collective-permute-done.late
  552.6 0.8 shard_map.110
Async XLA Ops:
  531.5 21.1 %collective-permute-start = (bf16[8,128,256]{2,1,0:T(8,128)(2,1)}, bf16[8,128,256]{2,1,0:T(8,128)(2,1)S(1)}, u32[]{:S(2)}, u32[]{:S(2)}) collective-permute-start(bf16[8,128,256]{2,1,0:T(8,128)(2,1)} %get-tuple-element.32), channel_id=1, source_target_pairs={{0,6},{1,7},{2,4},{3,5},{4,2},{5,3},{6,0},{7,1},{8,14},{9,15},{10,... | collective-permute-start | bytes 1572872 | tf_op jit(solution)/shard_map/ppermute | solution.py:466

commit v3 on v2

--- a/solution.py
+++ b/solution.py
@@ -9,7 +9,8 @@
 
 MESH = pl.DeviceIdType.MESH
 SLOTS = 6
-EARLY = (0, 1, 2, 0)
+EARLY = ((0, 0), (1, 1), (2, 2), (3, 0), (2, 1), (3, 2))
+SOON = 3
 
 
 def exchange(
@@ -48,9 +49,8 @@
             for i, (src, dst) in enumerate(((gate, in_gate), (up, in_up), (down, in_down)))
         ]
 
-    for t in range(2):
-        for copy in load(t):
-            copy.start()
+    for copy in load(0):
+        copy.start()
 
     barrier = pltpu.get_barrier_semaphore()
     for k in range(1, n):
@@ -109,20 +109,20 @@
     def block_of(ref, slot, d):
         return ref[slot, :, pl.ds(pl.multiple_of(d * cols, cols), cols)]
 
-    def raw_copy(r):
-        i = EARLY[r % len(EARLY)]
+    def raw_copy(j):
+        r, i = EARLY[j]
         d = at(1, r)[2]
         return pltpu.make_async_remote_copy(
             src_ref=(send_gate, send_up, send_down)[i].at[d],
-            dst_ref=raw_down.at[r] if i == 2 else raw_wide.at[r],
-            send_sem=raw_send.at[r],
-            recv_sem=raw_recv.at[r],
+            dst_ref=raw_down.at[j] if i == 2 else raw_wide.at[j],
+            send_sem=raw_send.at[j],
+            recv_sem=raw_recv.at[j],
             device_id={"shard": d},
             device_id_type=MESH,
         )
 
-    def raw_fill(r):
-        i = EARLY[r % len(EARLY)]
+    def raw_fill(j):
+        r, i = EARLY[j]
         d = at(1, r)[2]
         if i == 2:
             x = in_down[0, pl.ds(pl.multiple_of(d * cols, cols), cols), :]
@@ -133,26 +133,26 @@
     def down_factor(q, h, t):
         return jnp.broadcast_to(inverse[t, q, h, 2], (lanes, cols)).T
 
-    def raw_out_copy(r):
+    def raw_out_copy(j):
+        r, i = EARLY[j]
         s = at(1, half - r)[2]
-        i = EARLY[r % len(EARLY)]
         if i == 2:
             to = out_down.at[0, :, pl.ds(pl.multiple_of(s * inner, inner), inner)]
-            return pltpu.make_async_copy(raw_down.at[r], to, raw_out.at[r])
+            return pltpu.make_async_copy(raw_down.at[j], to, raw_out.at[j])
         to = (out_gate, out_up)[i].at[0, pl.ds(pl.multiple_of(s * rows, rows), rows), :]
-        return pltpu.make_async_copy(raw_wide.at[r], to, raw_out.at[r])
-
-    def raw_scale(r):
-        i = EARLY[r % len(EARLY)]
-        raw_copy(r).wait_recv()
+        return pltpu.make_async_copy(raw_wide.at[j], to, raw_out.at[j])
+
+    def raw_scale(j):
+        _, i = EARLY[j]
+        raw_copy(j).wait_recv()
         if i == 2:
             factor = down_factor(place, side, 0)
             for c in range(0, inner, lanes):
-                x = raw_down[r, :, c:c + lanes].astype(jnp.float32)
-                raw_down[r, :, c:c + lanes] = (x * factor).astype(jnp.bfloat16)
+                x = raw_down[j, :, c:c + lanes].astype(jnp.float32)
+                raw_down[j, :, c:c + lanes] = (x * factor).astype(jnp.bfloat16)
         else:
-            x = raw_wide[r].astype(jnp.float32)
-            raw_wide[r] = (x * inverse[0, place, side, i]).astype(jnp.bfloat16)
+            x = raw_wide[j].astype(jnp.float32)
+            raw_wide[j] = (x * inverse[0, place, side, i]).astype(jnp.bfloat16)
 
     def sums(t):
         slot = lax.rem(t, SLOTS)
@@ -228,7 +228,7 @@
         )):
             waiting = None
             for across, step in order + [(0, 0)]:
-                if first and across == 1 and EARLY[step % len(EARLY)] == i:
+                if first and across == 1 and (step, i) in EARLY:
                     continue
                 h, q, d = at(across, step)
                 to = t * n + d
@@ -290,8 +290,8 @@
 
         @pl.when(t == 2)
         def _():
-            for r in range(half // 2, half):
-                raw_copy(r).start()
+            for j in range(SOON, len(EARLY)):
+                raw_copy(j).start()
 
         @pl.when((t >= 2) & (t <= experts + 1))
         def _():
@@ -303,11 +303,11 @@
             for k in range(1, half):
                 router_relay(k).start()
             finish(0, True)
-            for r in range(half):
-                raw_scale(r)
-                if r:
-                    raw_out_copy(r - 1).start()
-            raw_out_copy(half - 1).start()
+            for j in range(len(EARLY)):
+                raw_scale(j)
+                if j:
+                    raw_out_copy(j - 1).start()
+            raw_out_copy(len(EARLY) - 1).start()
 
         @pl.when(t > 3)
         def _():
@@ -315,21 +315,24 @@
 
         return carry
 
-    for copy in load(2):
-        copy.start()
     for copy in load(0):
         copy.wait()
-    for r in range(half):
-        raw_fill(r)
+    for t in range(1, 3):
+        for copy in load(t):
+            copy.start()
     sums(0)
+    for j in range(SOON):
+        raw_fill(j)
     pl.semaphore_wait(barrier, n - 1 + groups - 1)
     share(0)
+    for j in range(SOON):
+        raw_copy(j).start()
     router_own.start()
     for k in range(1, half):
         router_first(0, k, 1).start()
     router_first(1, 0, 5).start()
-    for r in range(half // 2):
-        raw_copy(r).start()
+    for j in range(SOON, len(EARLY)):
+        raw_fill(j)
     lax.fori_loop(1, experts + 3, step, 0)
 
     gathered = out_router.at[router_rows, pl.ds(0, (n - 1) * depth)]
@@ -340,11 +343,11 @@
         router_second(k).start()
 
     pltpu.make_async_copy(later, later, later_sem).wait()
-    for r in range(half):
-        raw_copy(r).wait_send()
-        raw_out_copy(r).wait()
+    for j in range(len(EARLY)):
+        raw_copy(j).wait_send()
+        raw_out_copy(j).wait()
     for i, send in enumerate((send_gate, send_up, send_down)):
-        sent = experts * (n - 1) - sum(EARLY[r % len(EARLY)] == i for r in range(half))
+        sent = experts * (n - 1) - sum(j == i for _, j in EARLY)
         if i == 2:
             sent -= late
         blocks = send.at[pl.ds(0, sent)]
@@ -404,7 +407,7 @@
     cols = width // n
     inner = down.shape[2]
     depth, experts_here = router_weight.shape
-    if cols % 128 or inner % 128 or depth % 128 or n % 2 or n < 4 or experts < 8:
+    if cols % 128 or inner % 128 or depth % 128 or n % 2 or n < 8 or experts < 8:
         return by_collectives(gate, up, down, router_weight, router_gain)
     narrow, wide = jnp.bfloat16, jnp.float32
     half = n // 2
@@ -433,8 +436,8 @@
             pltpu.VMEM((experts * n, rows, cols), narrow),
             pltpu.VMEM((experts * n, rows, cols), narrow),
             pltpu.VMEM((experts * n, cols, inner), narrow),
-            pltpu.VMEM((half, rows, cols), narrow),
-            pltpu.VMEM((half, cols, inner), narrow),
+            pltpu.VMEM((len(EARLY), rows, cols), narrow),
+            pltpu.VMEM((len(EARLY), cols, inner), narrow),
             pltpu.VMEM((experts, half, 2, 3, 1, cols), wide),
             pltpu.VMEM((experts, half - 1, 2, 3, 1, cols), wide),
             pltpu.VMEM((experts, 2, 3, 1, cols), wide),
@@ -453,9 +456,9 @@
             dma((3,)),
             dma((3,)),
             dma,
-            dma((half,)),
-            dma((half,)),
-            dma((half,)),
+            dma((len(EARLY),)),
+            dma((len(EARLY),)),
+            dma((len(EARLY),)),
             dma((6,)),
         ],
         compiler_params=pltpu.CompilerParams(

time: 554 us -> 552 us (level)
  no operation moved by 1% of the time
where the time goes in v3:
time: 552 us
  Pallas kernels  550 us (100%)
    pallas_call x1, Pallas kernels, on_device(): pl.pallas_call(functools.partial(exchange, n, groups, late), out_shape=(j...  530 us
    pallas_call x1, Pallas kernels, on_device(): pl.pallas_call(place, in_specs=[any_space] * 3 + [vmem] * 4, out_specs=[a...  19.3 us
  transfers between devices with their start and end apart: 1, of which 0 were waited for; matrix products, arithmetic and copies ran while one was open for 0% of the time, Pallas kernels for 3%

profile of v3, /device:TPU:0, one launch (start us, length us, event | category | flops | bytes accessed | tf_op | source)
XLA Modules:
  0.0 551.9 jit_solution(3032960179529292320)
XLA Ops:
  0.6 529.8 %shard_map.108 = (bf16[16,2048,128]{2,1,0:T(8,128)(2,1)}, bf16[16,2048,128]{2,1,0:T(8,128)(2,1)}, bf16[16,128,2048]{2,1,0:T(8,128)(2,1)}, f32[16,128]{1,0:T(8,12...) custom-call(f32[16,256,1024]{2,1,0:T(8,128)} %gate.1, ...), custom_call_target="tpu_custom_call" | custom-call | tf_op jit(solution)/shard_map/pallas_call | solution.py:418
  530.4 1.3 collective-permute-start
  531.8 19.3 %shard_map.109 = (bf16[16,2048,128]{2,1,0:T(8,128)(2,1)}, bf16[16,2048,128]{2,1,0:T(8,128)(2,1)}, bf16[16,128,2048]{2,1,0:T(8,128)(2,1)}, f32[16,128]{1,0:T(8,12...) custom-call(bf16[16,2048,128]{2,1,0:T(8,128)(2,1)} %get-tuple-element.22.refs_0_, ...), custom_call_target="tpu_custom_call" | custom-call | bytes 50905088 | tf_op jit(solution)/shard_map/pallas_call | solution.py:474
  551.1 0.0 collective-permute-done.late
  551.1 0.8 shard_map.110
Async XLA Ops:
  530.4 20.7 %collective-permute-start = (bf16[8,128,256]{2,1,0:T(8,128)(2,1)}, bf16[8,128,256]{2,1,0:T(8,128)(2,1)S(1)}, u32[]{:S(2)}, u32[]{:S(2)}) collective-permute-start(bf16[8,128,256]{2,1,0:T(8,128)(2,1)} %get-tuple-element.32), channel_id=1, source_target_pairs={{0,6},{1,7},{2,4},{3,5},{4,2},{5,3},{6,0},{7,1},{8,14},{9,15},{10,... | collective-permute-start | bytes 1572872 | tf_op jit(solution)/shard_map/ppermute | solution.py:469

commit v4 on v3

--- a/solution.py
+++ b/solution.py
@@ -9,13 +9,14 @@
 
 MESH = pl.DeviceIdType.MESH
 SLOTS = 6
+HELD = 2
 EARLY = ((0, 0), (1, 1), (2, 2), (3, 0), (2, 1), (3, 2))
 SOON = 3
 
 
 def exchange(
-    n, groups, late, gate, up, down, weight, gain,
-    out_gate, out_up, out_down, scale_gate, scale_up, scale_down, out_router, later,
+    n, groups, late, late_outer, gate, up, down, weight, gain,
+    out_gate, out_up, out_down, scale_gate, scale_up, scale_down, out_router, later, later_outer,
     in_gate, in_up, in_down, send_gate, send_up, send_down, raw_wide, raw_down,
     part, arrived, mine, crossed, owned, inverse, narrow_router,
     load_sem, half_send, half_recv, cross_send, cross_recv, inv_send, inv_recv,
@@ -26,10 +27,12 @@
     inner = down.shape[2]
     half = n // 2
     first_late = experts - late
+    first_outer = experts - late_outer
     lanes = min(128, inner)
     me = lax.axis_index("shard")
     grp = lax.axis_index("expert")
     side, place = me // half, me % half
+    inner_one = side + place // (half // 2) == 1
 
     def at(across, step):
         there = lax.rem(side + across, 2)
@@ -255,21 +258,47 @@
                         device_id={"shard": d},
                         device_id_type=MESH,
                     )
-                    if i == 2 and (across, step) == (1, half // 2) and not first:
-                        @pl.when(t < first_late)
+                    if i < 2 and (across, step) == (1, half // 2) and not first:
+                        @pl.when(jnp.logical_not(inner_one & (t >= experts - HELD)))
                         def _():
                             copy.start()
-
-                        @pl.when(t >= first_late)
+                    elif i == 2 and (across, step) == (1, half // 2) and not first:
+                        kept = inner_one & (t >= first_late)
+                        kept_outer = jnp.logical_not(inner_one) & (t >= first_outer)
+
+                        @pl.when(jnp.logical_not(kept | kept_outer))
+                        def _():
+                            copy.start()
+
+                        @pl.when(kept)
                         def _():
                             pltpu.make_async_copy(
                                 send.at[to], later.at[t - first_late], later_sem
                             ).start()
+
+                        @pl.when(kept_outer)
+                        def _():
+                            pltpu.make_async_copy(
+                                send.at[to], later_outer.at[t - first_outer], later_sem
+                            ).start()
                     else:
                         copy.start()
 
                 waiting = go
             waiting()
+
+    def send_held():
+        d = at(1, half // 2)[2]
+        for t in range(experts - HELD, experts):
+            for i, (send, out) in enumerate(((send_gate, out_gate), (send_up, out_up))):
+                pltpu.make_async_remote_copy(
+                    src_ref=send.at[t * n + d],
+                    dst_ref=out.at[t, row_at, :],
+                    send_sem=big_send.at[i],
+                    recv_sem=big_recv.at[i],
+                    device_id={"shard": d},
+                    device_id_type=MESH,
+                ).start()
 
     def step(t, carry):
         @pl.when(t + 2 < experts)
@@ -335,6 +364,8 @@
         raw_fill(j)
     lax.fori_loop(1, experts + 3, step, 0)
 
+    pl.when(inner_one)(send_held)
+
     gathered = out_router.at[router_rows, pl.ds(0, (n - 1) * depth)]
     near = out_router.at[router_rows, pl.ds(0, (n - 2) * depth)]
     router_own.wait()
@@ -342,17 +373,28 @@
     for k in range(1, groups):
         router_second(k).start()
 
-    pltpu.make_async_copy(later, later, later_sem).wait()
     for j in range(len(EARLY)):
         raw_copy(j).wait_send()
         raw_out_copy(j).wait()
     for i, send in enumerate((send_gate, send_up, send_down)):
         sent = experts * (n - 1) - sum(j == i for _, j in EARLY)
+
+        def landed(sent, i=i, send=send):
+            blocks = send.at[pl.ds(0, sent)]
+            pltpu.make_async_copy(blocks, blocks, big_recv.at[i]).wait()
+            pltpu.make_async_copy(blocks, blocks, big_send.at[i]).wait()
+
         if i == 2:
-            sent -= late
-        blocks = send.at[pl.ds(0, sent)]
-        pltpu.make_async_copy(blocks, blocks, big_recv.at[i]).wait()
-        pltpu.make_async_copy(blocks, blocks, big_send.at[i]).wait()
+            for those, buffer, count in (
+                (inner_one, later, late),
+                (jnp.logical_not(inner_one), later_outer, late_outer),
+            ):
+                @pl.when(those)
+                def _(buffer=buffer, count=count, sent=sent, landed=landed):
+                    pltpu.make_async_copy(buffer, buffer, later_sem).wait()
+                    landed(sent - count)
+        else:
+            landed(sent)
         kept = send.at[pl.ds(0, experts)]
         pltpu.make_async_copy(kept, kept, own_sem.at[i]).wait()
     pltpu.make_async_copy(arrived, arrived, half_send).wait()
@@ -407,16 +449,16 @@
     cols = width // n
     inner = down.shape[2]
     depth, experts_here = router_weight.shape
-    if cols % 128 or inner % 128 or depth % 128 or n % 2 or n < 8 or experts < 8:
+    if cols % 128 or inner % 128 or depth % 128 or n % 4 or n < 8 or experts % 16:
         return by_collectives(gate, up, down, router_weight, router_gain)
     narrow, wide = jnp.bfloat16, jnp.float32
     half = n // 2
-    late = experts * 8 // 16
+    late, late_outer = experts * 12 // 16, experts * 4 // 16
     dma = pltpu.SemaphoreType.DMA
     any_space = pl.BlockSpec(memory_space=pl.ANY)
     vmem = pl.BlockSpec(memory_space=pltpu.VMEM)
     outs = pl.pallas_call(
-        functools.partial(exchange, n, groups, late),
+        functools.partial(exchange, n, groups, late, late_outer),
         out_shape=(
             jax.ShapeDtypeStruct((experts, rows * n, cols), narrow),
             jax.ShapeDtypeStruct((experts, rows * n, cols), narrow),
@@ -426,9 +468,10 @@
             jax.ShapeDtypeStruct((experts, cols), wide),
             jax.ShapeDtypeStruct((experts_here * groups, depth * n), narrow),
             jax.ShapeDtypeStruct((late, cols, inner), narrow),
+            jax.ShapeDtypeStruct((late_outer, cols, inner), narrow),
         ),
         in_specs=[any_space] * 3 + [vmem] * 2,
-        out_specs=(any_space,) * 3 + (vmem,) * 3 + (any_space,) * 2,
+        out_specs=(any_space,) * 3 + (vmem,) * 3 + (any_space,) * 3,
         scratch_shapes=[
             pltpu.VMEM((SLOTS, rows, width), wide),
             pltpu.VMEM((SLOTS, rows, width), wide),
@@ -465,9 +508,12 @@
             collective_id=0, has_side_effects=True, vmem_limit_bytes=60 * 2**20
         ),
     )(gate, up, down, router_weight.T, router_gain[None, :])
-    swap = [(d, n - half * (d // half + 1) + (d + half // 2) % half) for d in range(n)]
-    late_blocks = lax.ppermute(outs[7], "shard", swap)
-
+    swaps = [[], []]
+    for d in range(half):
+        to = half + (d + half // 2) % half
+        swaps[d < half // 2] += [(d, to), (to, d)]
+    late_blocks = lax.ppermute(outs[7], "shard", swaps[0])
+    outer_blocks = lax.ppermute(outs[8], "shard", swaps[1])
     big = [jax.ShapeDtypeStruct(x.shape, x.dtype) for x in outs[:3]]
     small = [jax.ShapeDtypeStruct(x.shape, x.dtype) for x in outs[3:7]]
     moved = sum(x.size * x.dtype.itemsize for x in outs[:7])
@@ -483,13 +529,13 @@
     )(*outs[:7])
     final_down = pl.pallas_call(
         functools.partial(place_late, n),
-        in_specs=[any_space] * 2,
+        in_specs=[any_space] * 3,
         out_specs=any_space,
         out_shape=jax.ShapeDtypeStruct(outs[2].shape, narrow),
         input_output_aliases={0: 0},
         scratch_shapes=[dma],
         compiler_params=pltpu.CompilerParams(vmem_limit_bytes=2**20),
-    )(placed[2], late_blocks)
+    )(placed[2], late_blocks, outer_blocks)
     return tuple(placed[:2]) + (final_down,) + tuple(placed[3:6]) + (placed[6].T,)
 
 
@@ -514,16 +560,21 @@
         give(t, i).wait()
 
 
-def place_late(n, _, late, out, sem):
-    count, _, inner = late.shape
+def place_late(n, _, late, late_outer, out, sem):
     me, half = lax.axis_index("shard"), n // 2
     source = (1 - me // half) * half + lax.rem(me + half // 2, half)
-    cols = pl.ds(pl.multiple_of(source * inner, inner), inner)
-    copy = pltpu.make_async_copy(
-        late, out.at[pl.ds(out.shape[0] - count, count), :, cols], sem
-    )
-    copy.start()
-    copy.wait()
+    inner_one = (me >= half // 2) & (me < half + half // 2)
+    for those, blocks in ((inner_one, late), (jnp.logical_not(inner_one), late_outer)):
+        count, _, inner = blocks.shape
+        cols = pl.ds(pl.multiple_of(source * inner, inner), inner)
+
+        @pl.when(those)
+        def _(blocks=blocks, count=count, cols=cols):
+            copy = pltpu.make_async_copy(
+                blocks, out.at[pl.ds(out.shape[0] - count, count), :, cols], sem
+            )
+            copy.start()
+            copy.wait()
 
 
 def solution(mesh):

time: 552 us -> 552 us (level)
  transfers between devices with their start and end apart: 1 -> 2, of which waited for: 0 -> 0; matrix products, arithmetic and copies ran while one was open for 0% -> 0% of each run, Pallas kernels for 3% -> 4%
where the time goes in v4:
time: 552 us; the launch traced here: 550 us
  Pallas kernels  545 us (99%)
    pallas_call x1, Pallas kernels, on_device(): pl.pallas_call(functools.partial(exchange, n, groups, late, late_outer),...  525 us
    pallas_call x1, Pallas kernels, on_device(): pl.pallas_call(place, in_specs=[any_space] * 3 + [vmem] * 4, out_specs=[a...  19.3 us
  transfers between devices with their start and end apart: 2, of which 0 were waited for; matrix products, arithmetic and copies ran while one was open for 0% of the time, Pallas kernels for 4%

profile of v4, /device:TPU:0, one launch (start us, length us, event | category | flops | bytes accessed | tf_op | source)
XLA Modules:
  0.0 549.8 jit_solution(15949319982279237231)
XLA Ops:
  0.6 525.1 %shard_map.108 = (bf16[16,2048,128]{2,1,0:T(8,128)(2,1)}, bf16[16,2048,128]{2,1,0:T(8,128)(2,1)}, bf16[16,128,2048]{2,1,0:T(8,128)(2,1)}, f32[16,128]{1,0:T(8,12...) custom-call(f32[16,256,1024]{2,1,0:T(8,128)} %gate.1, ...), custom_call_target="tpu_custom_call" | custom-call | tf_op jit(solution)/shard_map/pallas_call | solution.py:460
  525.8 0.7 collective-permute-start
  526.5 3.2 collective-permute-start.1
  529.8 19.3 %shard_map.109 = (bf16[16,2048,128]{2,1,0:T(8,128)(2,1)}, bf16[16,2048,128]{2,1,0:T(8,128)(2,1)}, bf16[16,128,2048]{2,1,0:T(8,128)(2,1)}, f32[16,128]{1,0:T(8,12...) custom-call(bf16[16,2048,128]{2,1,0:T(8,128)(2,1)} %get-tuple-element.23.refs_0_, ...), custom_call_target="tpu_custom_call" | custom-call | bytes 50905088 | tf_op jit(solution)/shard_map/pallas_call | solution.py:520
  549.1 0.0 collective-permute-done.1.late_outer
  549.1 0.0 collective-permute-done.late
  549.1 0.7 shard_map.110
Async XLA Ops:
  525.8 23.3 %collective-permute-start = (bf16[12,128,256]{2,1,0:T(8,128)(2,1)}, bf16[12,128,256]{2,1,0:T(8,128)(2,1)S(1)}, u32[]{:S(2)}, u32[]{:S(2)}) collective-permute-start(bf16[12,128,256]{2,1,0:T(8,128)(2,1)} %get-tuple-element.33), channel_id=1, source_target_pairs={{2,4},{4,2},{3,5},{5,3},{10,12},{12,10},{11,13},{13,11},{18,20},{2... | collective-permute-start | bytes 2359304 | tf_op jit(solution)/shard_map/ppermute | solution.py:515
  526.5 22.6 %collective-permute-start.1 = (bf16[4,128,256]{2,1,0:T(8,128)(2,1)}, bf16[4,128,256]{2,1,0:T(8,128)(2,1)S(1)}, u32[]{:S(2)}, u32[]{:S(2)}) collective-permute-start(bf16[4,128,256]{2,1,0:T(8,128)(2,1)} %get-tuple-element.34), channel_id=1, source_target_pairs={{0,6},{6,0},{1,7},{7,1},{8,14},{14,8},{9,15},{15,9},{16,22},{22,16... | collective-permute-start | bytes 786440 | tf_op jit(solution)/shard_map/ppermute | solution.py:516
